TPU v7x, 32 devices: a whole 2x2x4 slice. The times are simulated.
32 devices in a mesh: row: 4 (over y, x), col: 8 (over z, core).
Axes of the slice: x: 2, y: 2, z: 4, core: 2. Of those that a mesh axis runs over, the one named last changes fastest.
Arguments:
- grad_out: bfloat16 [512, 8192], P('col', 'row'), may hold values from -6 to 6
- weight: bfloat16 [28672, 8192], P('col', 'row'), may hold values from -0.0625 to 0.0625
Outputs:
- grad_in: bfloat16 [512, 28672], P('row', 'col')
All inputs are finite; a program needn't handle non-finite values.
Results may differ from a plain program's by a relative error of at most 0.001.
Values may be sent and summed in bfloat16 or wider, within the bound.
A program may use at most 64 MiB of HBM per device.

v0:
```python
import jax
import jax.numpy as jnp
from jax import lax
from jax.sharding import PartitionSpec as P


def contract(rows_block, weight):
    return lax.dot_general(
        rows_block, weight, (((1,), (1,)), ((), ())), preferred_element_type=jnp.float32
    )


def local(grad_out, weight):
    partial_value = contract(lax.all_gather(grad_out, "col", axis=0, tiled=True), weight)
    return lax.psum_scatter(partial_value, "row", scatter_dimension=0, tiled=True).astype(
        jnp.bfloat16
    )


def solution(mesh):
    return jax.shard_map(
        local,
        mesh=mesh,
        in_specs=(P("col", "row"), P("col", "row")),
        out_specs=P("row", "col"),
        check_vma=False,
    )
```

profile of v0, /device:TPU:0, one launch (start us, length us, event | category | flops | bytes accessed | tf_op | source)
XLA Modules:
  0.0 142.0 jit_solution(196821325022666454)
XLA Ops:
  6.5 0.0 all-gather.2.cloned.1.call-start
  6.5 0.7 all-gather.2.cloned.1.call-update
  7.3 0.0 reduce-scatter.2.cloned.1.call-start
  7.3 33.5 %all-gather.2.cloned.1.call-done = bf16[512,2048]{1,0:T(8,128)(2,1)} async-done(((bf16[64,2048]{1,0:T(8,128)(2,1)}), bf16[512,2048]{1,0:T(8,128)(2,1)}) %all-gather.2.cloned.1.call-update) | async-done | bytes 2097168 | tf_op jit(solution)/shard_map/all_gather | solution.py:14
  40.8 13.5 %fusion = f32[512,3584]{1,0:T(8,128)} fusion(bf16[512,2048]{1,0:T(8,128)(2,1)} %all-gather.2.cloned.1.call-done, bf16[3584,2048]{1,0:T(8,128)(2,1)} %param.3), kind=kOutput, calls=%fused_computation | convolution fusion | flops 7516192768 | bytes 24117248 | tf_op jit(solution)/shard_map/dot_general | solution.py:8
  54.4 0.0 reduce-scatter.2.cloned.1.call-update
  54.4 78.3 %reduce-scatter.2.cloned.1.call-done = f32[128,3584]{1,0:T(8,128)} async-done(((f32[512,3584]{1,0:T(8,128)}), f32[128,3584]{1,0:T(8,128)}) %reduce-scatter.2.cloned.1.call-update) | async-done | bytes 1835024 | tf_op jit(solution)/shard_map/reduce_scatter | solution.py:15
  132.7 2.5 %convert_element_type.3 = bf16[128,3584]{1,0:T(8,128)(2,1)} convert(f32[128,3584]{1,0:T(8,128)} %reduce-scatter.2.cloned.1.call-done) | non-fusion elementwise | flops 458752 | bytes 2752512 | tf_op jit(solution)/shard_map/convert_element_type | solution.py:15
Async XLA Ops:
  6.5 34.3 %all-gather.2.cloned.1.call-start = ((), (), s32[]{:S(2)}) async-start(), calls=%async_computation.1 | async-start | bytes 2359296 | tf_op jit(solution)/shard_map/all_gather | solution.py:14
  7.3 125.4 %reduce-scatter.2.cloned.1.call-start = ((), (), s32[]{:S(2)}) async-start(), calls=%async_computation.2 | async-start | bytes 9175040 | tf_op jit(solution)/shard_map/reduce_scatter | solution.py:15
Sparse Core Ops, SparseCore 0:
  8.9 31.8 all-gather.1
  54.5 78.1 reduce-scatter.1
where the time goes:
time: 142 us
  waiting for transfers between devices  113 us (80%)
  matrix products  13.5 us (10%)
  between operations  13.4 us (9%)
  other arithmetic  2.51 us (2%)
    reduce_scatter x1, waiting for transfers between devices, local(): lax.psum_scatter(partial_value, 'row', scatter_dimension=0, tiled=True)  78.3 us
    all_gather x1, waiting for transfers between devices, local(): lax.all_gather(grad_out, 'col', axis=0, tiled=True)  33.5 us
    dot_general x1, matrix products, contract(): lax.dot_general(rows_block, weight, (((1,), (1,)), ((), ())), preferred_e...  13.5 us
  transfers between devices with their start and end apart: 2, of which 2 were waited for; matrix products, arithmetic and copies ran while one was open for 0% of the time, Pallas kernels for 0%

commit v1 on v0

v1 whole, which is shorter than its diff:
```python
import functools

import jax
import jax.numpy as jnp
from jax import lax
from jax.experimental import pallas as pl
from jax.experimental.pallas import tpu as pltpu
from jax.sharding import PartitionSpec as P

MESH = pl.DeviceIdType.MESH
PHASES = 4
POWER = 13
TOP = 2.0**9.6
LOG2E = 1.4426950408889634


def contract(rows_block, weight):
    return lax.dot_general(
        rows_block, weight, (((1,), (1,)), ((), ())), preferred_element_type=jnp.float32
    )


def local_plain(grad_out, weight):
    partial_value = contract(lax.all_gather(grad_out, "col", axis=0, tiled=True), weight)
    return lax.psum_scatter(partial_value, "row", scatter_dimension=0, tiled=True).astype(
        jnp.bfloat16
    )


def encode(x, factor):
    y = x * factor
    y2 = y * y
    y4 = y2 * y2
    y8 = y4 * y4
    return (y8 * y4 * y).astype(jnp.bfloat16)


def decode(v, step):
    v = v.astype(jnp.float32)
    a = jnp.maximum(jnp.abs(v), 1e-37)
    y = jnp.exp2(jnp.log(a) * (LOG2E / POWER)) * step
    return jnp.where(v < 0, -y, y)


def kernel(
    Z, phases, chunk,
    g_ref, w_hbm, out_ref,
    w_ref, gbuf, acc, send1, send2, recv1, recv2, s_send, s_recv,
    w_sem, ag_send, ag_recv, fw_send, fw_recv, r_send, r_recv, q_send, q_recv,
):
    row = lax.axis_index("row")
    col = lax.axis_index("col")
    z, core = col // 2, col % 2
    rows = g_ref.shape[0] // phases
    ff, depth = w_hbm.shape
    half = ff // 2
    n_chunks = half // chunk
    partner = {"col": col + 1 - 2 * core}
    peers = [None]
    for k in range(1, Z):
        peers.append({"col": ((z + k) % Z) * 2 + core})
    x_row = row + 1 - 2 * (row % 2)
    y_row = (row + 2) % 4
    d_row = 3 - row
    link = [{"row": x_row}, {"row": y_row}]

    w_copies = []
    for i in range(2):
        for j in range(2):
            q = half // 2
            part = pl.ds(i * half + j * q, q)
            copy = pltpu.make_async_copy(w_hbm.at[part], w_ref.at[part], w_sem.at[2 * i + j])
            copy.start()
            w_copies.append(copy)

    barrier = pltpu.get_barrier_semaphore()
    targets = [partner] + peers[1:] + link
    for t in targets:
        pl.semaphore_signal(barrier, inc=1, device_id=t, device_id_type=MESH)
    pl.semaphore_wait(barrier, len(targets))

    def remote(src, dst, ssem, rsem, to):
        return pltpu.make_async_remote_copy(
            src_ref=src, dst_ref=dst, send_sem=ssem, recv_sem=rsem,
            device_id=to, device_id_type=MESH,
        )

    def shard_rows(s):
        return pl.ds(pl.multiple_of(s * rows, rows), rows)

    ag, own_fw, fw = {}, {}, {}
    for p in range(phases):
        src = g_ref.at[pl.ds(p * rows, rows)]
        dst = gbuf.at[p, shard_rows(col)]
        for k in range(1, Z):
            ag[p, k] = remote(src, dst, ag_send.at[p, k], ag_recv.at[p, k], peers[k])
            ag[p, k].start()
        own_fw[p] = remote(src, dst, fw_send.at[p, 0], fw_recv.at[p, 0], partner)
        own_fw[p].start()
    for p in range(phases):
        gbuf[p, shard_rows(col), :] = g_ref[pl.ds(p * rows, rows), :]

    def forward(p):
        for k in range(1, Z):
            ag[p, k].wait_recv()
            s = ((z + Z - k) % Z) * 2 + core
            block = gbuf.at[p, shard_rows(s)]
            fw[p, k] = remote(block, block, fw_send.at[p, k], fw_recv.at[p, k], partner)
            fw[p, k].start()

    def gathered(p):
        own_fw[p].wait_recv()
        for k in range(1, Z):
            fw[p, k].wait_recv()

    def matmul(p, i):
        @pl.loop(0, n_chunks)
        def _(j):
            at = pl.ds(pl.multiple_of(i * half + j * chunk, chunk), chunk)
            acc[p, :, :, at] = contract(gbuf[p], w_ref[at, :]).reshape(4, 2 * rows, chunk)

    def in_half(i, j):
        return pl.ds(pl.multiple_of(i * half + j * chunk, chunk), chunk)

    def local_cols(j):
        return pl.ds(pl.multiple_of(j * chunk, chunk), chunk)

    def put_scale(p, m, top):
        top = jnp.maximum(top, 1e-28)
        s_send[p, m] = jnp.broadcast_to(top * (1.0 / TOP), (8, 128))
        return TOP / top

    first, second, scales = {}, {}, {}

    def send_first(p, i):
        leaf = y_row if i == 0 else x_row
        to = link[1 - i]
        cols = pl.ds(i * half, half)
        top = jnp.maximum(
            jnp.max(jnp.abs(acc[p, d_row, :, cols]), keepdims=True),
            jnp.max(jnp.abs(acc[p, leaf, :, cols]), keepdims=True),
        )
        factor = put_scale(p, i, top)

        @pl.loop(0, n_chunks)
        def _(j):
            send1[p, i, 0, :, local_cols(j)] = encode(acc[p, d_row, :, in_half(i, j)], factor)
            send1[p, i, 1, :, local_cols(j)] = encode(acc[p, leaf, :, in_half(i, j)], factor)

        scales[p, i] = remote(
            s_send.at[p, i], s_recv.at[p, i], q_send.at[p, i], q_recv.at[p, i], to
        )
        scales[p, i].start()
        first[p, i] = remote(
            send1.at[p, i], recv1.at[p, i], r_send.at[p, i], r_recv.at[p, i], to
        )
        first[p, i].start()

    def combine(p, i):
        dest = x_row if i == 0 else y_row
        scales[p, i].wait_recv()
        first[p, i].wait_recv()
        step = s_recv[p, i][:1, :1]

        def add(j, top):
            total = acc[p, dest, :, in_half(i, j)] + decode(
                recv1[p, i, 0, :, local_cols(j)], step
            )
            acc[p, dest, :, in_half(i, j)] = total
            return jnp.maximum(top, jnp.max(jnp.abs(total), axis=0, keepdims=True))

        tops = lax.fori_loop(0, n_chunks, add, jnp.zeros((1, chunk), jnp.float32))
        factor = put_scale(p, 2 + i, jnp.max(tops, keepdims=True))

        @pl.loop(0, n_chunks)
        def _(j):
            send2[p, i, :, local_cols(j)] = encode(acc[p, dest, :, in_half(i, j)], factor)

        to = link[i]
        scales[p, 2 + i] = remote(
            s_send.at[p, 2 + i], s_recv.at[p, 2 + i], q_send.at[p, 2 + i], q_recv.at[p, 2 + i], to
        )
        scales[p, 2 + i].start()
        second[p, i] = remote(
            send2.at[p, i], recv2.at[p, i], r_send.at[p, 2 + i], r_recv.at[p, 2 + i], to
        )
        second[p, i].start()

    def finish(p, i):
        scales[p, 2 + i].wait_recv()
        second[p, i].wait_recv()
        step1 = s_recv[p, i][:1, :1]
        step2 = s_recv[p, 2 + i][:1, :1]
        span = g_ref.shape[0]

        @pl.loop(0, n_chunks)
        def _(j):
            total = (
                acc[p, row, :, in_half(i, j)]
                + decode(recv1[p, i, 1, :, local_cols(j)], step1)
                + decode(recv2[p, i, :, local_cols(j)], step2)
            ).astype(jnp.bfloat16)
            out_ref[pl.ds(p * rows, rows), in_half(i, j)] = total[:rows]
            out_ref[pl.ds(span + p * rows, rows), in_half(i, j)] = total[rows:]

    forward(0)
    for p in range(phases):
        gathered(p)
        for i in range(2):
            if p == 0:
                w_copies[2 * i].wait()
                w_copies[2 * i + 1].wait()
            matmul(p, i)
            send_first(p, i)
        if p + 1 < phases:
            forward(p + 1)
        if p >= 1:
            combine(p - 1, 0)
            combine(p - 1, 1)
        if p >= 2:
            finish(p - 2, 0)
            finish(p - 2, 1)
    last = phases - 1
    for i in range(2):
        combine(last, i)
    if last >= 1:
        for i in range(2):
            finish(last - 1, i)
    for i in range(2):
        finish(last, i)
    for copy in [*ag.values(), *own_fw.values(), *fw.values()]:
        copy.wait_send()
    for copy in [*first.values(), *second.values(), *scales.values()]:
        copy.wait_send()


def solution(mesh):
    n_row, n_col = mesh.shape["row"], mesh.shape["col"]

    def local(grad_out, weight):
        tokens, depth = grad_out.shape
        ff = weight.shape[0]
        phases = PHASES
        rows = tokens // phases
        chunk = 256
        fits = (
            n_row == 4
            and n_col == 2 * n_row
            and rows % 16 == 0
            and ff % (2 * chunk) == 0
            and depth % 128 == 0
        )
        if not fits:
            return local_plain(grad_out, weight)
        Z = n_col // 2
        half = ff // 2
        bf, f32 = jnp.bfloat16, jnp.float32
        dma = pltpu.SemaphoreType.DMA
        return pl.pallas_call(
            functools.partial(kernel, Z, phases, chunk),
            out_shape=jax.ShapeDtypeStruct((2 * tokens, ff), bf),
            in_specs=[
                pl.BlockSpec(memory_space=pltpu.VMEM),
                pl.BlockSpec(memory_space=pl.ANY),
            ],
            out_specs=pl.BlockSpec(memory_space=pltpu.VMEM),
            scratch_shapes=[
                pltpu.VMEM((ff, depth), bf),
                pltpu.VMEM((phases, n_col * rows, depth), bf),
                pltpu.VMEM((phases, 4, 2 * rows, ff), f32),
                pltpu.VMEM((phases, 2, 2, 2 * rows, half), bf),
                pltpu.VMEM((phases, 2, 2 * rows, half), bf),
                pltpu.VMEM((phases, 2, 2, 2 * rows, half), bf),
                pltpu.VMEM((phases, 2, 2 * rows, half), bf),
                pltpu.VMEM((phases, 4, 8, 128), f32),
                pltpu.VMEM((phases, 4, 8, 128), f32),
                dma((4,)),
                dma((phases, Z)),
                dma((phases, Z)),
                dma((phases, Z)),
                dma((phases, Z)),
                dma((phases, 4)),
                dma((phases, 4)),
                dma((phases, 4)),
                dma((phases, 4)),
            ],
            compiler_params=pltpu.CompilerParams(
                collective_id=0, has_side_effects=True, vmem_limit_bytes=56 * 1024 * 1024
            ),
        )(grad_out, weight)

    return jax.shard_map(
        local,
        mesh=mesh,
        in_specs=(P("col", "row"), P("col", "row")),
        out_specs=P("row", "col"),
        check_vma=False,
    )
```

time: 142 us -> 68.3 us (0.48)
  the two profiles are of different devices: /device:TPU:0 before, /device:TPU:8 now
where the time goes in v1:
time: 68.3 us; the launch traced here: 68.1 us
  Pallas kernels  65.9 us (96%)
  local copies, waits for them, and re-layouts  2.16 us (3%)
    pallas_call x1, Pallas kernels, local(): pl.pallas_call(functools.partial(kernel, Z, phases, chunk), out_shape=jax...  65.9 us
    unnamed x1, local copies, waits for them, and re-layouts  2.16 us

profile of v1, /device:TPU:8, one launch (start us, length us, event | category | flops | bytes accessed | tf_op | source)
XLA Modules:
  0.0 68.1 jit_solution(3246767427304388175)
XLA Ops:
  0.0 65.9 %shard_map.28 = bf16[128,3584]{1,0:T(8,128)(2,1)} custom-call(bf16[64,2048]{1,0:T(8,128)(2,1)} %g_ref.1, bf16[3584,2048]{1,0:T(8,128)(2,1)} %w_hbm.1), custom_call_target="tpu_custom_call" | custom-call | tf_op jit(solution)/shard_map/pallas_call | solution.py:259
  65.9 2.2 %copy.4 = bf16[128,3584]{1,0:T(8,128)(2,1)} copy(bf16[128,3584]{1,0:T(8,128)(2,1)} %shard_map.28) | data formatting | bytes 1835008

commit v2 on v1

v2 whole, which is shorter than its diff:
```python
import functools

import jax
import jax.numpy as jnp
from jax import lax
from jax.experimental import pallas as pl
from jax.experimental.pallas import tpu as pltpu
from jax.sharding import PartitionSpec as P

MESH = pl.DeviceIdType.MESH
SPLIT = (1, 1, 1, 1)
VMEM_BYTES = 48 * 1024 * 1024
POWER = 13
TOP = 2.0**9.6
LOG2E = 1.4426950408889634


def contract(rows_block, weight):
    return lax.dot_general(
        rows_block, weight, (((1,), (1,)), ((), ())), preferred_element_type=jnp.float32
    )


def local_plain(grad_out, weight):
    partial_value = contract(lax.all_gather(grad_out, "col", axis=0, tiled=True), weight)
    return lax.psum_scatter(partial_value, "row", scatter_dimension=0, tiled=True).astype(
        jnp.bfloat16
    )


def encode(x, factor):
    y = x * factor
    y2 = y * y
    y4 = y2 * y2
    y8 = y4 * y4
    return (y8 * y4 * y).astype(jnp.bfloat16)


def decode(v, step):
    v = v.astype(jnp.float32)
    a = jnp.maximum(jnp.abs(v), 1e-37)
    y = jnp.exp2(jnp.log(a) * (LOG2E / POWER)) * step
    return jnp.where(v < 0, -y, y)


def kernel(
    Z, split, chunk, wide,
    g_ref, w_hbm, out_ref, w_ref, s_send, s_recv,
    w_sem, ag_send, ag_recv, fw_send, fw_recv, r_send, r_recv, q_send, q_recv,
    *buffers,
):
    phases = len(split)
    gbuf, acc, send1, send2, recv1, recv2 = (
        buffers[n * phases : (n + 1) * phases] for n in range(6)
    )
    start_of = [sum(split[:p]) for p in range(phases)]
    row = lax.axis_index("row")
    col = lax.axis_index("col")
    z, core = col // 2, col % 2
    ff, depth = w_hbm.shape
    half = ff // 2
    n_chunks = half // chunk
    partner = {"col": col + 1 - 2 * core}
    low = jnp.minimum(z, Z - 1 - z)
    mirrored = z >= Z // 2
    others = []
    for i in range(Z - 1):
        t = i + (i >= low).astype(jnp.int32)
        others.append(jnp.where(mirrored, Z - 1 - t, t))
    at_end = low == 0
    near_end = jnp.where(mirrored, Z - 1, 0)
    x_row = row + 1 - 2 * (row % 2)
    y_row = (row + 2) % 4
    d_row = 3 - row
    link = [{"row": x_row}, {"row": y_row}]

    w_copies = []
    for i in range(2):
        for j in range(2):
            q = half // 2
            part = pl.ds(i * half + j * q, q)
            copy = pltpu.make_async_copy(w_hbm.at[part], w_ref.at[part], w_sem.at[2 * i + j])
            copy.start()
            w_copies.append(copy)

    def chip(t):
        return {"col": t * 2 + core}

    barrier = pltpu.get_barrier_semaphore()
    targets = [partner] + [chip(t) for t in others] + link
    for t in targets:
        pl.semaphore_signal(barrier, inc=1, device_id=t, device_id_type=MESH)
    pl.semaphore_wait(barrier, len(targets))

    def remote(src, dst, ssem, rsem, to):
        return pltpu.make_async_remote_copy(
            src_ref=src, dst_ref=dst, send_sem=ssem, recv_sem=rsem,
            device_id=to, device_id_type=MESH,
        )

    def shard_rows(p, s):
        return pl.ds(pl.multiple_of(s * split[p], split[p]), split[p])

    def own_to(p, i):
        return remote(
            g_ref.at[pl.ds(start_of[p], split[p])], gbuf[p].at[shard_rows(p, col)],
            ag_send.at[p, i], ag_recv.at[p, z], chip(others[i]),
        )

    def arrived(p, i):
        block = gbuf[p].at[shard_rows(p, others[i] * 2 + core)]
        return remote(block, block, ag_send.at[p, i], ag_recv.at[p, others[i]], chip(others[i]))

    own_fw, fw = {}, {}
    for p in range(phases):
        own_to(p, 0).start()
        own_to(p, 1).start()

        @pl.when(at_end)
        def _():
            own_to(p, 2).start()

        own_fw[p] = remote(
            g_ref.at[pl.ds(start_of[p], split[p])], gbuf[p].at[shard_rows(p, col)],
            fw_send.at[p, Z - 1], fw_recv.at[p, Z - 1], partner,
        )
        own_fw[p].start()
    for p in range(phases):
        gbuf[p][shard_rows(p, col), :] = g_ref[pl.ds(start_of[p], split[p]), :]

    def relay(p):
        @pl.when(jnp.logical_not(at_end))
        def _():
            arrived(p, 1).wait_recv()
            block = gbuf[p].at[shard_rows(p, others[1] * 2 + core)]
            remote(
                block, block, ag_send.at[p, 2], ag_recv.at[p, others[1]], chip(near_end)
            ).start()

    def forward(p):
        for i in range(Z - 1):
            if i == 1:
                @pl.when(at_end)
                def _():
                    arrived(p, 1).wait_recv()
            else:
                arrived(p, i).wait_recv()
            block = gbuf[p].at[shard_rows(p, others[i] * 2 + core)]
            fw[p, i] = remote(block, block, fw_send.at[p, i], fw_recv.at[p, i], partner)
            fw[p, i].start()

    def gathered(p):
        own_fw[p].wait_recv()
        for i in range(Z - 1):
            fw[p, i].wait_recv()

    def matmul(p, i):
        @pl.loop(0, half // wide)
        def _(j):
            at = pl.ds(pl.multiple_of(i * half + j * wide, wide), wide)
            product = contract(w_ref[at, :], gbuf[p][...])
            acc[p][:, :, at] = product.T.reshape(4, 2 * split[p], wide)

    def in_half(i, j):
        return pl.ds(pl.multiple_of(i * half + j * chunk, chunk), chunk)

    def local_cols(j):
        return pl.ds(pl.multiple_of(j * chunk, chunk), chunk)

    def put_scale(p, m, top):
        top = jnp.maximum(top, 1e-28)
        s_send[p, m] = jnp.broadcast_to(top * (1.0 / TOP), (8, 128))
        return TOP / top

    first, second, scales = {}, {}, {}

    def send_first(p, i):
        leaf = y_row if i == 0 else x_row
        to = link[1 - i]
        cols = pl.ds(i * half, half)
        top = jnp.maximum(
            jnp.max(jnp.abs(acc[p][d_row, :, cols]), keepdims=True),
            jnp.max(jnp.abs(acc[p][leaf, :, cols]), keepdims=True),
        )
        factor = put_scale(p, i, top)

        @pl.loop(0, n_chunks)
        def _(j):
            send1[p][i, 0, :, local_cols(j)] = encode(acc[p][d_row, :, in_half(i, j)], factor)
            send1[p][i, 1, :, local_cols(j)] = encode(acc[p][leaf, :, in_half(i, j)], factor)

        scales[p, i] = remote(
            s_send.at[p, i], s_recv.at[p, i], q_send.at[p, i], q_recv.at[p, i], to
        )
        scales[p, i].start()
        first[p, i] = remote(
            send1[p].at[i], recv1[p].at[i], r_send.at[p, i], r_recv.at[p, i], to
        )
        first[p, i].start()

    def combine(p, i):
        dest = x_row if i == 0 else y_row
        scales[p, i].wait_recv()
        first[p, i].wait_recv()
        step = s_recv[p, i][:1, :1]

        def add(j, top):
            total = acc[p][dest, :, in_half(i, j)] + decode(
                recv1[p][i, 0, :, local_cols(j)], step
            )
            acc[p][dest, :, in_half(i, j)] = total
            return jnp.maximum(top, jnp.max(jnp.abs(total), axis=0, keepdims=True))

        tops = lax.fori_loop(0, n_chunks, add, jnp.zeros((1, chunk), jnp.float32))
        factor = put_scale(p, 2 + i, jnp.max(tops, keepdims=True))

        @pl.loop(0, n_chunks)
        def _(j):
            send2[p][i, :, local_cols(j)] = encode(acc[p][dest, :, in_half(i, j)], factor)

        to = link[i]
        scales[p, 2 + i] = remote(
            s_send.at[p, 2 + i], s_recv.at[p, 2 + i], q_send.at[p, 2 + i], q_recv.at[p, 2 + i], to
        )
        scales[p, 2 + i].start()
        second[p, i] = remote(
            send2[p].at[i], recv2[p].at[i], r_send.at[p, 2 + i], r_recv.at[p, 2 + i], to
        )
        second[p, i].start()

    def finish(p, i):
        scales[p, 2 + i].wait_recv()
        second[p, i].wait_recv()
        step1 = s_recv[p, i][:1, :1]
        step2 = s_recv[p, 2 + i][:1, :1]
        span = g_ref.shape[0]

        @pl.loop(0, n_chunks)
        def _(j):
            total = (
                acc[p][row, :, in_half(i, j)]
                + decode(recv1[p][i, 1, :, local_cols(j)], step1)
                + decode(recv2[p][i, :, local_cols(j)], step2)
            ).astype(jnp.bfloat16)
            out_ref[pl.ds(start_of[p], split[p]), in_half(i, j)] = total[: split[p]]
            out_ref[pl.ds(span + start_of[p], split[p]), in_half(i, j)] = total[split[p] :]

    relay(0)
    forward(0)
    for p in range(phases):
        gathered(p)
        for i in range(2):
            if p == 0:
                w_copies[2 * i].wait()
                w_copies[2 * i + 1].wait()
            matmul(p, i)
            send_first(p, i)
            if p + 1 < phases and i == 0:
                relay(p + 1)
        if p + 1 < phases:
            forward(p + 1)
        if p >= 1:
            combine(p - 1, 0)
            combine(p - 1, 1)
        if p >= 2:
            finish(p - 2, 0)
            finish(p - 2, 1)
    last = phases - 1
    for i in range(2):
        combine(last, i)
    if last >= 1:
        for i in range(2):
            finish(last - 1, i)
    for i in range(2):
        finish(last, i)
    for p in range(phases):
        for i in range(Z - 1):
            own_to(p, i).wait_send()
    for copy in [*own_fw.values(), *fw.values()]:
        copy.wait_send()
    for copy in [*first.values(), *second.values(), *scales.values()]:
        copy.wait_send()


def solution(mesh):
    n_row, n_col = mesh.shape["row"], mesh.shape["col"]

    def local(grad_out, weight):
        tokens, depth = grad_out.shape
        ff = weight.shape[0]
        quarter = tokens // 4
        split = tuple(quarter * n for n in SPLIT)
        chunk = 256
        fits = (
            n_row == 4
            and n_col == 2 * n_row
            and quarter % 16 == 0
            and ff % (2 * chunk) == 0
            and depth % 128 == 0
        )
        if not fits:
            return local_plain(grad_out, weight)
        Z = n_col // 2
        half = ff // 2
        wide = half // 2
        phases = len(split)
        bf, f32 = jnp.bfloat16, jnp.float32
        dma = pltpu.SemaphoreType.DMA
        return pl.pallas_call(
            functools.partial(kernel, Z, split, chunk, wide),
            out_shape=jax.ShapeDtypeStruct((2 * tokens, ff), bf),
            in_specs=[
                pl.BlockSpec(memory_space=pltpu.VMEM),
                pl.BlockSpec(memory_space=pl.ANY),
            ],
            out_specs=pl.BlockSpec(memory_space=pltpu.VMEM),
            scratch_shapes=[
                pltpu.VMEM((ff, depth), bf),
                pltpu.VMEM((phases, 4, 8, 128), f32),
                pltpu.VMEM((phases, 4, 8, 128), f32),
                dma((4,)),
                *[dma((phases, Z))] * 4,
                *[dma((phases, 4))] * 4,
                *[pltpu.VMEM((n_col * n, depth), bf) for n in split],
                *[pltpu.VMEM((4, 2 * n, ff), f32) for n in split],
                *[pltpu.VMEM((2, 2, 2 * n, half), bf) for n in split],
                *[pltpu.VMEM((2, 2 * n, half), bf) for n in split],
                *[pltpu.VMEM((2, 2, 2 * n, half), bf) for n in split],
                *[pltpu.VMEM((2, 2 * n, half), bf) for n in split],
            ],
            compiler_params=pltpu.CompilerParams(
                collective_id=0, has_side_effects=True, vmem_limit_bytes=VMEM_BYTES
            ),
        )(grad_out, weight)

    return jax.shard_map(
        local,
        mesh=mesh,
        in_specs=(P("col", "row"), P("col", "row")),
        out_specs=P("row", "col"),
        check_vma=False,
    )
```

time: 68.3 us -> 59.5 us (0.87)
  the two profiles are of different devices: /device:TPU:8 before, /device:TPU:0 now
where the time goes in v2:
time: 59.5 us; the launch traced here: 59.3 us
  Pallas kernels  57.4 us (96%)
  local copies, waits for them, and re-layouts  1.87 us (3%)
    pallas_call x1, Pallas kernels, local(): pl.pallas_call(functools.partial(kernel, Z, split, chunk, wide), out_shap...  57.4 us
    unnamed x3, local copies, waits for them, and re-layouts  1.87 us

profile of v2, /device:TPU:0, one launch (start us, length us, event | category | flops | bytes accessed | tf_op | source)
XLA Modules:
  0.0 59.3 jit_solution(12730550367811901006)
XLA Ops:
  0.0 0.0 copy-start
  0.0 0.9 %copy-done = bf16[64,2048]{1,0:T(8,128)(2,1)S(1)} copy-done((bf16[64,2048]{1,0:T(8,128)(2,1)S(1)}, bf16[64,2048]{1,0:T(8,128)(2,1)}, u32[]{:S(2)}) %copy-start) | copy-done | bytes 262168
  1.0 57.4 %shard_map.28 = bf16[128,3584]{1,0:T(8,128)(2,1)S(1)} custom-call(bf16[64,2048]{1,0:T(8,128)(2,1)S(1)} %copy-done, bf16[3584,2048]{1,0:T(8,128)(2,1)} %w_hbm.1), custom_call_target="tpu_custom_call" | custom-call | tf_op jit(solution)/shard_map/pallas_call | solution.py:309
  58.4 0.9 %copy.4 = bf16[128,3584]{1,0:T(8,128)(2,1)} copy(bf16[128,3584]{1,0:T(8,128)(2,1)S(1)} %shard_map.28) | data formatting | bytes 1835008
Async XLA Ops:
  0.0 0.9 %copy-start = (bf16[64,2048]{1,0:T(8,128)(2,1)S(1)}, bf16[64,2048]{1,0:T(8,128)(2,1)}, u32[]{:S(2)}) copy-start(bf16[64,2048]{1,0:T(8,128)(2,1)} %g_ref.1) | copy-start | bytes 786436

commit v3 on v2

--- a/solution.py
+++ b/solution.py
@@ -9,6 +9,7 @@
 
 MESH = pl.DeviceIdType.MESH
 SPLIT = (1, 1, 1, 1)
+PARTS = (1, 1, 1, 1)
 VMEM_BYTES = 48 * 1024 * 1024
 POWER = 13
 TOP = 2.0**9.6
@@ -28,8 +29,26 @@
     )
 
 
+def fold_max(x):
+    x = jnp.abs(x)
+    tiles = [
+        x[a : a + 8, b : b + 128]
+        for a in range(0, x.shape[0], 8)
+        for b in range(0, x.shape[1], 128)
+    ]
+    while len(tiles) > 1:
+        odd = tiles[-1:] if len(tiles) % 2 else []
+        tiles = [jnp.maximum(s, t) for s, t in zip(tiles[::2], tiles[1::2])] + odd
+    return tiles[0]
+
+
+def spread(tile, shape):
+    line = jnp.concatenate([tile] * (shape[1] // 128), axis=1)
+    return jnp.concatenate([line] * (shape[0] // 8), axis=0)
+
+
 def encode(x, factor):
-    y = x * factor
+    y = x * spread(factor, x.shape)
     y2 = y * y
     y4 = y2 * y2
     y8 = y4 * y4
@@ -39,12 +58,12 @@
 def decode(v, step):
     v = v.astype(jnp.float32)
     a = jnp.maximum(jnp.abs(v), 1e-37)
-    y = jnp.exp2(jnp.log(a) * (LOG2E / POWER)) * step
+    y = jnp.exp2(jnp.log(a) * (LOG2E / POWER)) * spread(step, v.shape)
     return jnp.where(v < 0, -y, y)
 
 
 def kernel(
-    Z, split, chunk, wide,
+    Z, split, parts, chunk, wide,
     g_ref, w_hbm, out_ref, w_ref, s_send, s_recv,
     w_sem, ag_send, ag_recv, fw_send, fw_recv, r_send, r_recv, q_send, q_recv,
     *buffers,
@@ -59,7 +78,7 @@
     z, core = col // 2, col % 2
     ff, depth = w_hbm.shape
     half = ff // 2
-    n_chunks = half // chunk
+    most = max(parts)
     partner = {"col": col + 1 - 2 * core}
     low = jnp.minimum(z, Z - 1 - z)
     mirrored = z >= Z // 2
@@ -112,9 +131,10 @@
         return remote(block, block, ag_send.at[p, i], ag_recv.at[p, others[i]], chip(others[i]))
 
     own_fw, fw = {}, {}
-    for p in range(phases):
+
+    def issue(p):
+        own_to(p, 1).start()
         own_to(p, 0).start()
-        own_to(p, 1).start()
 
         @pl.when(at_end)
         def _():
@@ -125,6 +145,8 @@
             fw_send.at[p, Z - 1], fw_recv.at[p, Z - 1], partner,
         )
         own_fw[p].start()
+
+    issue(0)
     for p in range(phases):
         gbuf[p][shard_rows(p, col), :] = g_ref[pl.ds(start_of[p], split[p]), :]
 
@@ -154,40 +176,50 @@
         for i in range(Z - 1):
             fw[p, i].wait_recv()
 
+    def width(p):
+        return half // parts[p]
+
+    def base(p, i):
+        return i % 2 * half + i // 2 * width(p)
+
     def matmul(p, i):
-        @pl.loop(0, half // wide)
+        @pl.loop(0, width(p) // wide)
         def _(j):
-            at = pl.ds(pl.multiple_of(i * half + j * wide, wide), wide)
+            at = pl.ds(pl.multiple_of(base(p, i) + j * wide, wide), wide)
             product = contract(w_ref[at, :], gbuf[p][...])
             acc[p][:, :, at] = product.T.reshape(4, 2 * split[p], wide)
 
-    def in_half(i, j):
-        return pl.ds(pl.multiple_of(i * half + j * chunk, chunk), chunk)
+    def in_half(p, i, j):
+        return pl.ds(pl.multiple_of(base(p, i) + j * chunk, chunk), chunk)
 
     def local_cols(j):
         return pl.ds(pl.multiple_of(j * chunk, chunk), chunk)
 
     def put_scale(p, m, top):
         top = jnp.maximum(top, 1e-28)
-        s_send[p, m] = jnp.broadcast_to(top * (1.0 / TOP), (8, 128))
+        s_send[p, m] = top * (1.0 / TOP)
         return TOP / top
 
     first, second, scales = {}, {}, {}
 
     def send_first(p, i):
-        leaf = y_row if i == 0 else x_row
-        to = link[1 - i]
-        cols = pl.ds(i * half, half)
-        top = jnp.maximum(
-            jnp.max(jnp.abs(acc[p][d_row, :, cols]), keepdims=True),
-            jnp.max(jnp.abs(acc[p][leaf, :, cols]), keepdims=True),
-        )
+        leaf = y_row if i % 2 == 0 else x_row
+        to = link[1 - i % 2]
+
+        def largest(j, top):
+            cols = in_half(p, i, j)
+            return jnp.maximum(
+                top,
+                jnp.maximum(fold_max(acc[p][d_row, :, cols]), fold_max(acc[p][leaf, :, cols])),
+            )
+
+        top = lax.fori_loop(0, width(p) // chunk, largest, jnp.zeros((8, 128), jnp.float32))
         factor = put_scale(p, i, top)
 
-        @pl.loop(0, n_chunks)
+        @pl.loop(0, width(p) // chunk)
         def _(j):
-            send1[p][i, 0, :, local_cols(j)] = encode(acc[p][d_row, :, in_half(i, j)], factor)
-            send1[p][i, 1, :, local_cols(j)] = encode(acc[p][leaf, :, in_half(i, j)], factor)
+            send1[p][i, 0, :, local_cols(j)] = encode(acc[p][d_row, :, in_half(p, i, j)], factor)
+            send1[p][i, 1, :, local_cols(j)] = encode(acc[p][leaf, :, in_half(p, i, j)], factor)
 
         scales[p, i] = remote(
             s_send.at[p, i], s_recv.at[p, i], q_send.at[p, i], q_recv.at[p, i], to
@@ -199,79 +231,85 @@
         first[p, i].start()
 
     def combine(p, i):
-        dest = x_row if i == 0 else y_row
+        dest = x_row if i % 2 == 0 else y_row
         scales[p, i].wait_recv()
         first[p, i].wait_recv()
-        step = s_recv[p, i][:1, :1]
+        step = s_recv[p, i]
 
         def add(j, top):
-            total = acc[p][dest, :, in_half(i, j)] + decode(
+            total = acc[p][dest, :, in_half(p, i, j)] + decode(
                 recv1[p][i, 0, :, local_cols(j)], step
             )
-            acc[p][dest, :, in_half(i, j)] = total
-            return jnp.maximum(top, jnp.max(jnp.abs(total), axis=0, keepdims=True))
-
-        tops = lax.fori_loop(0, n_chunks, add, jnp.zeros((1, chunk), jnp.float32))
-        factor = put_scale(p, 2 + i, jnp.max(tops, keepdims=True))
-
-        @pl.loop(0, n_chunks)
+            acc[p][dest, :, in_half(p, i, j)] = total
+            return jnp.maximum(top, fold_max(total))
+
+        tops = lax.fori_loop(0, width(p) // chunk, add, jnp.zeros((8, 128), jnp.float32))
+        factor = put_scale(p, 2 * most + i, tops)
+
+        @pl.loop(0, width(p) // chunk)
         def _(j):
-            send2[p][i, :, local_cols(j)] = encode(acc[p][dest, :, in_half(i, j)], factor)
-
-        to = link[i]
-        scales[p, 2 + i] = remote(
-            s_send.at[p, 2 + i], s_recv.at[p, 2 + i], q_send.at[p, 2 + i], q_recv.at[p, 2 + i], to
-        )
-        scales[p, 2 + i].start()
+            send2[p][i, :, local_cols(j)] = encode(acc[p][dest, :, in_half(p, i, j)], factor)
+
+        to = link[i % 2]
+        scales[p, 2 * most + i] = remote(
+            s_send.at[p, 2 * most + i], s_recv.at[p, 2 * most + i], q_send.at[p, 2 * most + i], q_recv.at[p, 2 * most + i], to
+        )
+        scales[p, 2 * most + i].start()
         second[p, i] = remote(
-            send2[p].at[i], recv2[p].at[i], r_send.at[p, 2 + i], r_recv.at[p, 2 + i], to
+            send2[p].at[i], recv2[p].at[i], r_send.at[p, 2 * most + i], r_recv.at[p, 2 * most + i], to
         )
         second[p, i].start()
 
     def finish(p, i):
-        scales[p, 2 + i].wait_recv()
+        scales[p, 2 * most + i].wait_recv()
         second[p, i].wait_recv()
-        step1 = s_recv[p, i][:1, :1]
-        step2 = s_recv[p, 2 + i][:1, :1]
+        step1 = s_recv[p, i]
+        step2 = s_recv[p, 2 * most + i]
         span = g_ref.shape[0]
 
-        @pl.loop(0, n_chunks)
+        @pl.loop(0, width(p) // chunk)
         def _(j):
             total = (
-                acc[p][row, :, in_half(i, j)]
+                acc[p][row, :, in_half(p, i, j)]
                 + decode(recv1[p][i, 1, :, local_cols(j)], step1)
                 + decode(recv2[p][i, :, local_cols(j)], step2)
             ).astype(jnp.bfloat16)
-            out_ref[pl.ds(start_of[p], split[p]), in_half(i, j)] = total[: split[p]]
-            out_ref[pl.ds(span + start_of[p], split[p]), in_half(i, j)] = total[split[p] :]
+            out_ref[pl.ds(start_of[p], split[p]), in_half(p, i, j)] = total[: split[p]]
+            out_ref[pl.ds(span + start_of[p], split[p]), in_half(p, i, j)] = total[split[p] :]
 
     relay(0)
+    if phases > 1:
+        issue(1)
     forward(0)
     for p in range(phases):
         gathered(p)
-        for i in range(2):
-            if p == 0:
-                w_copies[2 * i].wait()
-                w_copies[2 * i + 1].wait()
+        for i in range(2 * parts[p]):
+            if p == 0 and i < 2 * parts[0]:
+                if i < 2:
+                    w_copies[2 * i].wait()
+                if i // 2 == parts[0] - 1:
+                    w_copies[2 * (i % 2) + 1].wait()
             matmul(p, i)
             send_first(p, i)
             if p + 1 < phases and i == 0:
                 relay(p + 1)
+                if p + 2 < phases:
+                    issue(p + 2)
         if p + 1 < phases:
             forward(p + 1)
         if p >= 1:
-            combine(p - 1, 0)
-            combine(p - 1, 1)
+            for i in range(2 * parts[p - 1]):
+                combine(p - 1, i)
         if p >= 2:
-            finish(p - 2, 0)
-            finish(p - 2, 1)
+            for i in range(2 * parts[p - 2]):
+                finish(p - 2, i)
     last = phases - 1
-    for i in range(2):
+    for i in range(2 * parts[last]):
         combine(last, i)
     if last >= 1:
-        for i in range(2):
+        for i in range(2 * parts[last - 1]):
             finish(last - 1, i)
-    for i in range(2):
+    for i in range(2 * parts[last]):
         finish(last, i)
     for p in range(phases):
         for i in range(Z - 1):
@@ -290,12 +328,12 @@
         ff = weight.shape[0]
         quarter = tokens // 4
         split = tuple(quarter * n for n in SPLIT)
-        chunk = 256
+        chunk = ff // 4
         fits = (
             n_row == 4
             and n_col == 2 * n_row
             and quarter % 16 == 0
-            and ff % (2 * chunk) == 0
+            and ff % 512 == 0
             and depth % 128 == 0
         )
         if not fits:
@@ -307,7 +345,7 @@
         bf, f32 = jnp.bfloat16, jnp.float32
         dma = pltpu.SemaphoreType.DMA
         return pl.pallas_call(
-            functools.partial(kernel, Z, split, chunk, wide),
+            functools.partial(kernel, Z, split, PARTS, chunk, wide),
             out_shape=jax.ShapeDtypeStruct((2 * tokens, ff), bf),
             in_specs=[
                 pl.BlockSpec(memory_space=pltpu.VMEM),
@@ -316,17 +354,17 @@
             out_specs=pl.BlockSpec(memory_space=pltpu.VMEM),
             scratch_shapes=[
                 pltpu.VMEM((ff, depth), bf),
-                pltpu.VMEM((phases, 4, 8, 128), f32),
-                pltpu.VMEM((phases, 4, 8, 128), f32),
+                pltpu.VMEM((phases, 4 * max(PARTS), 8, 128), f32),
+                pltpu.VMEM((phases, 4 * max(PARTS), 8, 128), f32),
                 dma((4,)),
                 *[dma((phases, Z))] * 4,
-                *[dma((phases, 4))] * 4,
+                *[dma((phases, 4 * max(PARTS)))] * 4,
                 *[pltpu.VMEM((n_col * n, depth), bf) for n in split],
                 *[pltpu.VMEM((4, 2 * n, ff), f32) for n in split],
-                *[pltpu.VMEM((2, 2, 2 * n, half), bf) for n in split],
-                *[pltpu.VMEM((2, 2 * n, half), bf) for n in split],
-                *[pltpu.VMEM((2, 2, 2 * n, half), bf) for n in split],
-                *[pltpu.VMEM((2, 2 * n, half), bf) for n in split],
+                *[pltpu.VMEM((2 * k, 2, 2 * n, half // k), bf) for n, k in zip(split, PARTS)],
+                *[pltpu.VMEM((2 * k, 2 * n, half // k), bf) for n, k in zip(split, PARTS)],
+                *[pltpu.VMEM((2 * k, 2, 2 * n, half // k), bf) for n, k in zip(split, PARTS)],
+                *[pltpu.VMEM((2 * k, 2 * n, half // k), bf) for n, k in zip(split, PARTS)],
             ],
             compiler_params=pltpu.CompilerParams(
                 collective_id=0, has_side_effects=True, vmem_limit_bytes=VMEM_BYTES

time: 59.5 us -> 55.9 us (0.939)
  Pallas kernels: 57.4 us -> 53.9 us
    pallas_call x1, Pallas kernels: 57.4 us -> 53.9 us  [local(): pl.pallas_call(functools.partial(kernel, Z, split, PARTS, chunk, wide), o...]
where the time goes in v3:
time: 55.9 us; the launch traced here: 55.8 us
  Pallas kernels  53.9 us (96%)
  local copies, waits for them, and re-layouts  1.87 us (3%)
    pallas_call x1, Pallas kernels, local(): pl.pallas_call(functools.partial(kernel, Z, split, PARTS, chunk, wide), o...  53.9 us
    unnamed x3, local copies, waits for them, and re-layouts  1.87 us

profile of v3, /device:TPU:0, one launch (start us, length us, event | category | flops | bytes accessed | tf_op | source)
XLA Modules:
  0.0 55.8 jit_solution(3138908791483350670)
XLA Ops:
  0.0 0.0 copy-start
  0.0 0.9 %copy-done = bf16[64,2048]{1,0:T(8,128)(2,1)S(1)} copy-done((bf16[64,2048]{1,0:T(8,128)(2,1)S(1)}, bf16[64,2048]{1,0:T(8,128)(2,1)}, u32[]{:S(2)}) %copy-start) | copy-done | bytes 262168
  1.0 53.9 %shard_map.28 = bf16[128,3584]{1,0:T(8,128)(2,1)S(1)} custom-call(bf16[64,2048]{1,0:T(8,128)(2,1)S(1)} %copy-done, bf16[3584,2048]{1,0:T(8,128)(2,1)} %w_hbm.1), custom_call_target="tpu_custom_call" | custom-call | tf_op jit(solution)/shard_map/pallas_call | solution.py:347
  54.9 0.9 %copy.4 = bf16[128,3584]{1,0:T(8,128)(2,1)} copy(bf16[128,3584]{1,0:T(8,128)(2,1)S(1)} %shard_map.28) | data formatting | bytes 1835008
Async XLA Ops:
  0.0 0.9 %copy-start = (bf16[64,2048]{1,0:T(8,128)(2,1)S(1)}, bf16[64,2048]{1,0:T(8,128)(2,1)}, u32[]{:S(2)}) copy-start(bf16[64,2048]{1,0:T(8,128)(2,1)} %g_ref.1) | copy-start | bytes 786436

commit v4 on v3

--- a/solution.py
+++ b/solution.py
@@ -64,8 +64,8 @@
 
 def kernel(
     Z, split, parts, chunk, wide,
-    g_ref, w_hbm, out_ref, w_ref, s_send, s_recv,
-    w_sem, ag_send, ag_recv, fw_send, fw_recv, r_send, r_recv, q_send, q_recv,
+    g_ref, w_hbm, out_ref, w_ref,
+    w_sem, ag_send, ag_recv, fw_send, fw_recv, r_send, r_recv,
     *buffers,
 ):
     phases = len(split)
@@ -192,15 +192,32 @@
     def in_half(p, i, j):
         return pl.ds(pl.multiple_of(base(p, i) + j * chunk, chunk), chunk)
 
-    def local_cols(j):
-        return pl.ds(pl.multiple_of(j * chunk, chunk), chunk)
-
-    def put_scale(p, m, top):
-        top = jnp.maximum(top, 1e-28)
-        s_send[p, m] = top * (1.0 / TOP)
-        return TOP / top
-
-    first, second, scales = {}, {}, {}
+    def step_of(top):
+        step = jnp.maximum(top, 1e-28) * (1.0 / TOP)
+        return jnp.concatenate([step, step], axis=0).astype(jnp.bfloat16)
+
+    def factor_of(step):
+        return 1.0 / step.astype(jnp.float32)[:8]
+
+    def at_group(j, k, high, offset, count):
+        start = j * (chunk // 128 * high) + (k * high + offset)
+        return pl.ds(pl.multiple_of(start, 16), count)
+
+    def store_coded(ref, i, j, high, offset, value):
+        for k in range(chunk // 128):
+            rows = at_group(j, k, high, offset, value.shape[0])
+            ref[i, rows, :] = value[:, k * 128 : (k + 1) * 128]
+
+    def load_coded(ref, i, j, high, offset, count):
+        return jnp.concatenate(
+            [ref[i, at_group(j, k, high, offset, count), :] for k in range(chunk // 128)],
+            axis=1,
+        )
+
+    def step_rows(p, high):
+        return pl.ds(width(p) // 128 * high, 16)
+
+    first, second = {}, {}
 
     def send_first(p, i):
         leaf = y_row if i % 2 == 0 else x_row
@@ -214,17 +231,18 @@
             )
 
         top = lax.fori_loop(0, width(p) // chunk, largest, jnp.zeros((8, 128), jnp.float32))
-        factor = put_scale(p, i, top)
+        step = step_of(top)
+        factor = factor_of(step)
+        n = 2 * split[p]
+        send1[p][i, step_rows(p, 2 * n), :] = step
 
         @pl.loop(0, width(p) // chunk)
         def _(j):
-            send1[p][i, 0, :, local_cols(j)] = encode(acc[p][d_row, :, in_half(p, i, j)], factor)
-            send1[p][i, 1, :, local_cols(j)] = encode(acc[p][leaf, :, in_half(p, i, j)], factor)
-
-        scales[p, i] = remote(
-            s_send.at[p, i], s_recv.at[p, i], q_send.at[p, i], q_recv.at[p, i], to
-        )
-        scales[p, i].start()
+            far = encode(acc[p][d_row, :, in_half(p, i, j)], factor)
+            store_coded(send1[p], i, j, 2 * n, 0, far)
+            near = encode(acc[p][leaf, :, in_half(p, i, j)], factor)
+            store_coded(send1[p], i, j, 2 * n, n, near)
+
         first[p, i] = remote(
             send1[p].at[i], recv1[p].at[i], r_send.at[p, i], r_recv.at[p, i], to
         )
@@ -232,47 +250,46 @@
 
     def combine(p, i):
         dest = x_row if i % 2 == 0 else y_row
-        scales[p, i].wait_recv()
         first[p, i].wait_recv()
-        step = s_recv[p, i]
+        n = 2 * split[p]
+        step = recv1[p][i, step_rows(p, 2 * n), :].astype(jnp.float32)[:8]
 
         def add(j, top):
             total = acc[p][dest, :, in_half(p, i, j)] + decode(
-                recv1[p][i, 0, :, local_cols(j)], step
+                load_coded(recv1[p], i, j, 2 * n, 0, n), step
             )
             acc[p][dest, :, in_half(p, i, j)] = total
             return jnp.maximum(top, fold_max(total))
 
         tops = lax.fori_loop(0, width(p) // chunk, add, jnp.zeros((8, 128), jnp.float32))
-        factor = put_scale(p, 2 * most + i, tops)
+        new_step = step_of(tops)
+        factor = factor_of(new_step)
+        send2[p][i, step_rows(p, n), :] = new_step
 
         @pl.loop(0, width(p) // chunk)
         def _(j):
-            send2[p][i, :, local_cols(j)] = encode(acc[p][dest, :, in_half(p, i, j)], factor)
+            coded = encode(acc[p][dest, :, in_half(p, i, j)], factor)
+            store_coded(send2[p], i, j, n, 0, coded)
 
         to = link[i % 2]
-        scales[p, 2 * most + i] = remote(
-            s_send.at[p, 2 * most + i], s_recv.at[p, 2 * most + i], q_send.at[p, 2 * most + i], q_recv.at[p, 2 * most + i], to
-        )
-        scales[p, 2 * most + i].start()
         second[p, i] = remote(
             send2[p].at[i], recv2[p].at[i], r_send.at[p, 2 * most + i], r_recv.at[p, 2 * most + i], to
         )
         second[p, i].start()
 
     def finish(p, i):
-        scales[p, 2 * most + i].wait_recv()
         second[p, i].wait_recv()
-        step1 = s_recv[p, i]
-        step2 = s_recv[p, 2 * most + i]
+        n = 2 * split[p]
+        step1 = recv1[p][i, step_rows(p, 2 * n), :].astype(jnp.float32)[:8]
+        step2 = recv2[p][i, step_rows(p, n), :].astype(jnp.float32)[:8]
         span = g_ref.shape[0]
 
         @pl.loop(0, width(p) // chunk)
         def _(j):
             total = (
                 acc[p][row, :, in_half(p, i, j)]
-                + decode(recv1[p][i, 1, :, local_cols(j)], step1)
-                + decode(recv2[p][i, :, local_cols(j)], step2)
+                + decode(load_coded(recv1[p], i, j, 2 * n, n, n), step1)
+                + decode(load_coded(recv2[p], i, j, n, 0, n), step2)
             ).astype(jnp.bfloat16)
             out_ref[pl.ds(start_of[p], split[p]), in_half(p, i, j)] = total[: split[p]]
             out_ref[pl.ds(span + start_of[p], split[p]), in_half(p, i, j)] = total[split[p] :]
@@ -316,7 +333,7 @@
             own_to(p, i).wait_send()
     for copy in [*own_fw.values(), *fw.values()]:
         copy.wait_send()
-    for copy in [*first.values(), *second.values(), *scales.values()]:
+    for copy in [*first.values(), *second.values()]:
         copy.wait_send()
 
 
@@ -354,17 +371,15 @@
             out_specs=pl.BlockSpec(memory_space=pltpu.VMEM),
             scratch_shapes=[
                 pltpu.VMEM((ff, depth), bf),
-                pltpu.VMEM((phases, 4 * max(PARTS), 8, 128), f32),
-                pltpu.VMEM((phases, 4 * max(PARTS), 8, 128), f32),
                 dma((4,)),
                 *[dma((phases, Z))] * 4,
-                *[dma((phases, 4 * max(PARTS)))] * 4,
+                *[dma((phases, 4 * max(PARTS)))] * 2,
                 *[pltpu.VMEM((n_col * n, depth), bf) for n in split],
                 *[pltpu.VMEM((4, 2 * n, ff), f32) for n in split],
-                *[pltpu.VMEM((2 * k, 2, 2 * n, half // k), bf) for n, k in zip(split, PARTS)],
-                *[pltpu.VMEM((2 * k, 2 * n, half // k), bf) for n, k in zip(split, PARTS)],
-                *[pltpu.VMEM((2 * k, 2, 2 * n, half // k), bf) for n, k in zip(split, PARTS)],
-                *[pltpu.VMEM((2 * k, 2 * n, half // k), bf) for n, k in zip(split, PARTS)],
+                *[pltpu.VMEM((2 * k, half // k // 128 * 4 * n + 16, 128), bf) for n, k in zip(split, PARTS)],
+                *[pltpu.VMEM((2 * k, half // k // 128 * 2 * n + 16, 128), bf) for n, k in zip(split, PARTS)],
+                *[pltpu.VMEM((2 * k, half // k // 128 * 4 * n + 16, 128), bf) for n, k in zip(split, PARTS)],
+                *[pltpu.VMEM((2 * k, half // k // 128 * 2 * n + 16, 128), bf) for n, k in zip(split, PARTS)],
             ],
             compiler_params=pltpu.CompilerParams(
                 collective_id=0, has_side_effects=True, vmem_limit_bytes=VMEM_BYTES

time: 55.9 us -> 55.6 us (level)
  no operation moved by 1% of the time
where the time goes in v4:
time: 55.6 us; the launch traced here: 55.5 us
  Pallas kernels  53.6 us (96%)
  local copies, waits for them, and re-layouts  1.87 us (3%)
    pallas_call x1, Pallas kernels, local(): pl.pallas_call(functools.partial(kernel, Z, split, PARTS, chunk, wide), o...  53.6 us
    unnamed x3, local copies, waits for them, and re-layouts  1.87 us

profile of v4, /device:TPU:0, one launch (start us, length us, event | category | flops | bytes accessed | tf_op | source)
XLA Modules:
  0.0 55.5 jit_solution(364302058907413501)
XLA Ops:
  0.0 0.0 copy-start
  0.0 0.9 %copy-done = bf16[64,2048]{1,0:T(8,128)(2,1)S(1)} copy-done((bf16[64,2048]{1,0:T(8,128)(2,1)S(1)}, bf16[64,2048]{1,0:T(8,128)(2,1)}, u32[]{:S(2)}) %copy-start) | copy-done | bytes 262168
  1.0 53.6 %shard_map.28 = bf16[128,3584]{1,0:T(8,128)(2,1)S(1)} custom-call(bf16[64,2048]{1,0:T(8,128)(2,1)S(1)} %copy-done, bf16[3584,2048]{1,0:T(8,128)(2,1)} %w_hbm.1), custom_call_target="tpu_custom_call" | custom-call | tf_op jit(solution)/shard_map/pallas_call | solution.py:364
  54.6 0.9 %copy.4 = bf16[128,3584]{1,0:T(8,128)(2,1)} copy(bf16[128,3584]{1,0:T(8,128)(2,1)S(1)} %shard_map.28) | data formatting | bytes 1835008
Async XLA Ops:
  0.0 0.9 %copy-start = (bf16[64,2048]{1,0:T(8,128)(2,1)S(1)}, bf16[64,2048]{1,0:T(8,128)(2,1)}, u32[]{:S(2)}) copy-start(bf16[64,2048]{1,0:T(8,128)(2,1)} %g_ref.1) | copy-start | bytes 786436
